TPU v7x, 256 devices: a whole 4x4x8 slice. The times are simulated.
256 devices in a mesh: role: 2 (over core), wide: 8 (over x_hi, y), tp: 16 (over z, x_lo).
Axes of the slice: x: 4 (x_hi: 2, x_lo: 2; x = x_hi * 2 + x_lo), y: 4, z: 8, core: 2. Of those that a mesh axis runs over, the one named last changes fastest.
Arguments:
- normed: bfloat16 [4096, 4096], P('wide', ('role', 'tp')), may hold values from -0.29882812 to 0.29882812
- queries: bfloat16 [4096, 4096], P('wide', 'tp'), may hold values from -4 to 4
- keys: bfloat16 [4096, 1024], P('wide'), may hold values from -4 to 4
- values: bfloat16 [4096, 1024], P('wide'), may hold values from -6 to 6
- attn_out: bfloat16 [4096, 4096], P('wide', 'tp'), may hold values from -0.29882812 to 0.29882812
- row_logsumexp: float32 [32, 4096], P('tp'), as said below
- out_grad: bfloat16 [4096, 4096], P('wide', ('role', 'tp')), may hold values from -6 to 6
- out_weight: bfloat16 [4096, 4096], P('tp'), may hold values from -0.09375 to 0.09375
- qkv_weight: bfloat16 [4096, 6144], P(('role', 'tp')), may hold values from -0.09375 to 0.09375
- documents: int32 [4096], replicated, may hold values from 0 to 2, as said below
- tasks: int32 [8, 16, 2], replicated, may hold values from -1 to 15, as said below
Outputs:
- normed_grad: bfloat16 [4096, 4096], P('wide', ('role', 'tp'))
- out_weight_grad: bfloat16 [4096, 4096], P('tp', ('role', 'wide'))
- qkv_weight_grad: bfloat16 [4096, 6144], P(('role', 'tp'), 'wide')
Inputs may be any that keep to these rules, and one draw needn't show every extreme that they name: `documents`: document numbers never fall along the tokens, and every number from 0 to 2 is used. `tasks`: row s lists in its first slots the query blocks of server s, in [s, j, 0], followed by slots holding -1 in both places; every query block from 0 to 15 stands in exactly one slot of the table; [s, j, 1] is the block holding the first token of the document of the query block's first token. row_logsumexp[h, i] is the logarithm of the sum, over the tokens j that token i may attend, of exp(scores[h, i, j]) as computed from queries and keys.
All inputs are finite; a program needn't handle non-finite values.
Results may differ from a plain program's by a relative error of at most 0.018.
Values may be sent and summed in bfloat16 or wider, within the bound.
A program may use at most 128 MiB of HBM per device.

v0:
```python
import jax
import jax.numpy as jnp
from jax import lax
from jax.sharding import PartitionSpec as P

D = 4096
QUERY_HEADS = 32
KEY_VALUE_HEADS = 8
HEAD_SIZE = 128


def cut_along(shard, dim, length):
    before, after = (shard.shape[:dim], shard.shape[dim + 1 :])
    return jnp.moveaxis(shard.reshape(*before, length, -1, *after), dim, 0)


def sum_at_owner(shard, axis, dim):
    tiles = cut_along(shard, dim, lax.axis_size(axis))
    arrived = lax.all_to_all(tiles, axis, split_axis=0, concat_axis=0, tiled=True)
    return arrived.astype(jnp.float32).sum(axis=0)


def in_one_piece(arrays, axis, dim, along):
    both = jnp.concatenate(arrays, axis=along)
    out, at, done = (lax.all_gather(both, axis, axis=dim, tiled=True), 0, [])
    for a in arrays:
        done.append(lax.slice_in_dim(out, at, at + a.shape[along], axis=along))
        at += a.shape[along]
    return tuple(done)


def local(
    normed,
    queries,
    keys,
    values,
    attn_out,
    row_logsumexp,
    out_grad,
    out_weight,
    qkv_weight,
    documents,
    tasks,
):
    role_pos = lax.axis_index("role")
    is_worker = role_pos == 0
    wide_count = lax.axis_size("wide")
    wide_pos = lax.axis_index("wide")
    tp_pos = lax.axis_index("tp")
    local_rows = normed.shape[0]
    row_halves = local_rows // 2
    head_count = queries.shape[1] // HEAD_SIZE
    pair_count = head_count // 2
    kv_count = max(1, head_count // 4)
    score_scale = HEAD_SIZE ** (-0.5)
    total_rows = wide_count * local_rows
    block_count = tasks.shape[1]
    full_grad = lax.all_gather(out_grad, ("role", "tp"), axis=1, tiled=True)
    grad_half = lax.dynamic_slice_in_dim(full_grad, role_pos * (D // 2), D // 2, 1)
    out_part = lax.dot_general(
        attn_out, grad_half, (((0,), (0,)), ((), ())), preferred_element_type=jnp.float32
    )
    out_sum = sum_at_owner(out_part.astype(jnp.bfloat16), "wide", 1)

    def worker_side():
        return lax.dot_general(
            full_grad, out_weight, (((1,), (1,)), ((), ())), preferred_element_type=jnp.float32
        ).astype(jnp.bfloat16)

    def server_side():
        return queries

    first_piece = lax.cond(is_worker, worker_side, server_side)
    kv_start = tp_pos * head_count // 4 * HEAD_SIZE
    key_cols = lax.dynamic_slice_in_dim(keys, kv_start, kv_count * HEAD_SIZE, 1)
    value_cols = lax.dynamic_slice_in_dim(values, kv_start, kv_count * HEAD_SIZE, 1)
    kv_piece = jnp.where(is_worker, key_cols, value_cols)
    out_piece = lax.dynamic_slice_in_dim(
        attn_out, role_pos * pair_count * HEAD_SIZE, pair_count * HEAD_SIZE, 1
    )
    gathered = in_one_piece((first_piece, kv_piece, out_piece), ("role", "wide"), 0, 1)
    grad_all = gathered[0][:total_rows]
    query_all = gathered[0][total_rows:]
    key_all = gathered[1][:total_rows]
    value_all = gathered[1][total_rows:]
    output_all = gathered[2].reshape(2, total_rows, pair_count, HEAD_SIZE)
    delta_all = jnp.einsum(
        "irpd,ripd->rpi",
        grad_all.reshape(total_rows, 2, pair_count, HEAD_SIZE),
        output_all,
        preferred_element_type=jnp.float32,
    ).reshape(pair_count, 2, total_rows)
    lse_all = row_logsumexp.reshape(pair_count, 2, total_rows)

    def tile(block_q, block_k, query_grad, kv_acc):
        offsets = jnp.arange(row_halves, dtype=jnp.int32)
        query_pos = block_q * row_halves + offsets
        key_pos = block_k * row_halves + offsets
        query_rows = lax.dynamic_slice_in_dim(
            query_all, block_q * row_halves, row_halves, 0
        ).reshape(row_halves, pair_count, 2, HEAD_SIZE)
        grad_rows = lax.dynamic_slice_in_dim(grad_all, block_q * row_halves, row_halves, 0).reshape(
            row_halves, pair_count, 2, HEAD_SIZE
        )
        key_rows = lax.dynamic_slice_in_dim(key_all, block_k * row_halves, row_halves, 0).reshape(
            row_halves, kv_count, HEAD_SIZE
        )
        value_rows = lax.dynamic_slice_in_dim(
            value_all, block_k * row_halves, row_halves, 0
        ).reshape(row_halves, kv_count, HEAD_SIZE)
        lse_rows = lax.dynamic_slice_in_dim(lse_all, block_q * row_halves, row_halves, 2)
        delta_rows = lax.dynamic_slice_in_dim(delta_all, block_q * row_halves, row_halves, 2)
        query_docs = lax.dynamic_slice_in_dim(documents, block_q * row_halves, row_halves, 0)
        key_docs = lax.dynamic_slice_in_dim(documents, block_k * row_halves, row_halves, 0)
        allowed = (query_docs[:, None] == key_docs[None, :]) & (
            key_pos[None, :] <= query_pos[:, None]
        )
        scores = (
            jnp.einsum("qphd,cpd->phqc", query_rows, key_rows, preferred_element_type=jnp.float32)
            * score_scale
        )
        probs = jnp.exp(jnp.where(allowed, scores - lse_rows[..., None], -jnp.inf))
        probs_low = probs.astype(jnp.bfloat16)
        value_grad = jnp.einsum(
            "phqc,qphd->cpd", probs_low, grad_rows, preferred_element_type=jnp.float32
        )
        prob_grad = jnp.einsum(
            "qphd,cpd->phqc", grad_rows, value_rows, preferred_element_type=jnp.float32
        )
        score_grad = (probs * (prob_grad - delta_rows[..., None]) * score_scale).astype(
            jnp.bfloat16
        )
        query_tile = jnp.einsum(
            "phqc,cpd->qphd", score_grad, key_rows, preferred_element_type=jnp.float32
        )
        query_grad = query_grad + query_tile.reshape(row_halves, head_count * HEAD_SIZE)
        key_grad = jnp.einsum(
            "phqc,qphd->cpd", score_grad, query_rows, preferred_element_type=jnp.float32
        )
        tile_kv = jnp.concatenate([key_grad, value_grad], axis=2).reshape(
            row_halves, pair_count * 2 * HEAD_SIZE
        )
        target = block_k % 2 * wide_count + block_k // 2
        current = lax.dynamic_index_in_dim(kv_acc, target, 0, keepdims=False)
        kv_acc = lax.dynamic_update_index_in_dim(kv_acc, current + tile_kv, target, 0)
        return (query_grad, kv_acc)

    def empty_side():
        return (
            jnp.zeros((block_count, row_halves, head_count * HEAD_SIZE), jnp.float32),
            jnp.zeros((block_count, row_halves, pair_count * 2 * HEAD_SIZE), jnp.float32),
        )

    def attend_side():
        own_row = lax.dynamic_index_in_dim(tasks, wide_pos, 0, keepdims=False)

        def slot_turn(number, carry):
            query_acc, kv_acc = carry
            block_q = own_row[number, 0]
            valid = block_q >= 0
            safe_q = jnp.maximum(block_q, 0)
            upper = jnp.where(valid, safe_q + 1, 0)
            lower = jnp.where(valid, own_row[number, 1], 0)

            def key_turn(block_k, inner):
                return tile(safe_q, block_k, inner[0], inner[1])

            start = jnp.zeros((row_halves, head_count * HEAD_SIZE), jnp.float32)
            query_grad, kv_acc = lax.fori_loop(lower, upper, key_turn, (start, kv_acc))
            target = safe_q % 2 * wide_count + safe_q // 2
            current = lax.dynamic_index_in_dim(query_acc, target, 0, keepdims=False)
            query_acc = lax.dynamic_update_index_in_dim(query_acc, current + query_grad, target, 0)
            return (query_acc, kv_acc)

        return lax.fori_loop(0, block_count, slot_turn, empty_side())

    query_acc, kv_acc = lax.cond(is_worker, empty_side, attend_side)
    kv_flat = kv_acc.reshape(block_count * row_halves, pair_count * 2 * HEAD_SIZE)
    kv_sum = sum_at_owner(kv_flat.astype(jnp.bfloat16), ("role", "wide"), 0)
    arrived = lax.all_to_all(
        query_acc.astype(jnp.bfloat16), ("role", "wide"), split_axis=0, concat_axis=0, tiled=True
    )
    query_piece = jnp.sum(arrived.astype(jnp.float32), axis=0).astype(jnp.bfloat16)
    head_q, key_value_head = in_one_piece(
        (query_piece, kv_sum.astype(jnp.bfloat16)), ("role", "tp"), 1, 0
    )
    query_grads = head_q.reshape(row_halves, 2, QUERY_HEADS * HEAD_SIZE)
    grouped_queries = jnp.sum(
        key_value_head.reshape(row_halves, 2, KEY_VALUE_HEADS, 2, 2 * HEAD_SIZE).astype(
            jnp.float32
        ),
        axis=3,
    ).astype(jnp.bfloat16)
    key_gradients = grouped_queries[..., :HEAD_SIZE].reshape(
        row_halves, 2, KEY_VALUE_HEADS * HEAD_SIZE
    )
    value_gradients = grouped_queries[..., HEAD_SIZE:].reshape(
        row_halves, 2, KEY_VALUE_HEADS * HEAD_SIZE
    )
    qkv_grads = jnp.concatenate([query_grads, key_gradients, value_gradients], axis=2)
    normed_grad = jnp.einsum(
        "irc,nc->rin", qkv_grads, qkv_weight, preferred_element_type=jnp.float32
    )
    normed_grad = normed_grad.reshape(local_rows, qkv_weight.shape[0]).astype(jnp.bfloat16)
    qkv_part = jnp.einsum(
        "rin,irc->nc",
        normed.reshape(2, row_halves, normed.shape[1]),
        qkv_grads,
        preferred_element_type=jnp.float32,
    )
    qkv_sum = sum_at_owner(qkv_part.astype(jnp.bfloat16), "wide", 1)
    return (normed_grad, out_sum.astype(jnp.bfloat16), qkv_sum.astype(jnp.bfloat16))


def solution(mesh):
    in_specs = (
        P("wide", ("role", "tp")),
        P("wide", "tp"),
        P("wide", None),
        P("wide", None),
        P("wide", "tp"),
        P("tp", None),
        P("wide", ("role", "tp")),
        P("tp", None),
        P(("role", "tp"), None),
        P(),
        P(),
    )
    out_specs = (P("wide", ("role", "tp")), P("tp", ("role", "wide")), P(("role", "tp"), "wide"))
    return jax.shard_map(local, mesh=mesh, in_specs=in_specs, out_specs=out_specs, check_vma=False)
```

profile of v0, /device:TPU:1, one launch (start us, length us, event | category | flops | bytes accessed | tf_op | source)
XLA Modules:
  0.0 605.2 jit_solution(3537214650441579339)
XLA Ops:
  10.3 75.8 %all-gather.4.cloned.1.call-done = bf16[512,4096]{1,0:T(8,128)(2,1)} async-done(((bf16[512,128]{1,0:T(8,128)(2,1)}), bf16[512,4096]{1,0:T(8,128)(2,1)}) %all-gather.4.cloned.1.call-update) | async-done | bytes 4194320 | tf_op jit(solution)/shard_map/all_gather | solution.py:58
  88.1 83.6 %all-gather.6.cloned.1.call-done = bf16[8192,512]{0,1:T(8,128)(2,1)} async-done(((bf16[512,512]{0,1:T(8,128)(2,1)}), bf16[8192,512]{0,1:T(8,128)(2,1)}) %all-gather.6.cloned.1.call-update) | async-done | bytes 8388624 | tf_op jit(solution)/shard_map/all_gather | solution.py:25
  171.8 3.2 slice.52
  174.9 4.1 convert.5
  179.0 214.2 %conditional.3 = (f32[16,256,256]{1,2,0:T(8,128)}, f32[16,256,256]{1,2,0:T(8,128)}) conditional(s32[]{:T(128)} %convert_element_type.57, (s32[]{:T(128)}, s32[8,16,2]{1,2,0:T(2,128)}, s32[4096]{0:T(1024)}, bf16[8192,512]{0,1:T(8,128)(2,1)}, f32[2,4096]{1,0:T(2,128)}, /*index=5*/bf16[4096,256]{0,1:T(8,128)(2,1)}, f32[2,4096,128]{1,2,0:T(8,128)}, ...), branch_computations={%region_2.7_spmd.clone, %region_7.8_spmd} | conditional | flops 172417568 | bytes 72474416 | solution.py:177
  179.7 3.2 slice.49
  182.8 4.5 reshape.193
  187.3 6.8 %fusion.23 = f32[2,4096]{1,0:T(2,128)S(1)} fusion(bf16[2,4096,128]{1,0,2:T(2,128)(2,1)} %reshape.193, f32[2,4096,128]{1,2,0:T(8,128)} %get-tuple-element.631), kind=kLoop, calls=%fused_computation.43 | loop fusion | flops 3137536 | bytes 6324224 | tf_op jit(solution)/shard_map/irpd,ripd->rpi/dot_general | solution.py:87
  194.1 3.1 slice.46
  197.3 11.6 %copy.83 = bf16[8192,512]{1,0:T(8,128)(2,1)} copy(bf16[8192,512]{0,1:T(8,128)(2,1)} %get-tuple-element.632) | data formatting | bytes 16777216 | tf_op jit(solution)/shard_map
  210.2 11.6 %copy.82 = bf16[8192,512]{1,0:T(8,128)(2,1)} copy(bf16[8192,512]{0,1:T(8,128)(2,1)} %get-tuple-element.632) | data formatting | bytes 16777216 | tf_op jit(solution)/shard_map
  224.2 2.4 broadcast.52.clone
  226.6 2.4 broadcast.52
  229.0 164.3 %while.56 = (s32[]{:T(128)}, f32[16,256,256]{1,2,0:T(8,128)}, f32[16,256,256]{1,2,0:T(8,128)}, s32[16,2]{0,1:T(2,128)S(1)}, s32[4096]{0:T(1024)}, /*index=5*/bf1...) while((s32[]{:T(128)}, f32[16,256,256]{1,2,0:T(8,128)}, ...), condition=%wide.region_6.6_spmd, body=%wide.region_3.5_spmd.sunk | while | flops 169280032 | bytes 7429371 | solution.py:175
  235.0 55.2 %while.57 = (s32[]{:T(128)}, f32[256,256]{0,1:T(8,128)S(1)}, f32[16,256,256]{1,2,0:T(8,128)}, s32[]{:T(128)}, bf16[4096,128]{1,0:T(8,128)(2,1)}, /*index=5*/s32[...) while((s32[]{:T(128)}, f32[256,256]{0,1:T(8,128)S(1)}, ...), condition=%wide.region_5.4_spmd, body=%wide.region_4.3_spmd.sunk | while | flops 169214464 | bytes 5321220 | solution.py:169
  393.2 3.8 convert_element_type.58
  397.0 4.3 all-to-all-start
  401.4 3.8 convert_element_type.59
  405.1 23.5 %all-to-all-done = bf16[16,256,256]{1,2,0:T(8,128)(2,1)} async-done(((bf16[16,256,256]{1,2,0:T(8,128)(2,1)}), bf16[16,256,256]{1,2,0:T(8,128)(2,1)}, u32[]{:S(2)}, u32[]{:S(2)}) %all-to-all-start) | async-done | bytes 2097184 | tf_op jit(solution)/shard_map/all_to_all | solution.py:180
  428.6 4.5 all-to-all-start.1
  435.2 26.9 %all-to-all-done.1 = bf16[16,256,256]{1,2,0:T(8,128)(2,1)} async-done(((bf16[16,256,256]{1,2,0:T(8,128)(2,1)}), bf16[16,256,256]{1,2,0:T(8,128)(2,1)}, u32[]{:S(2)}, u32[]{:S(2)}) %all-to-all-start.1) | async-done | bytes 2097184 | tf_op jit(solution)/shard_map/all_to_all | solution.py:19
  464.8 3.3 convolution_convert_fusion.1
  468.1 3.7 all-to-all-start.2
  471.8 67.4 %all-gather.8.cloned.1.call-done = bf16[512,8192]{0,1:T(8,128)(2,1)} async-done(((bf16[512,256]{0,1:T(8,128)(2,1)}), bf16[512,8192]{0,1:T(8,128)(2,1)}) %all-gather.8.cloned.1.call-update) | async-done | bytes 8388624 | tf_op jit(solution)/shard_map/all_gather | solution.py:25
  539.2 5.7 fusion.34
  544.9 6.4 %copy.60 = bf16[256,2,4096]{2,0,1:T(8,128)(2,1)} copy(bf16[256,2,4096]{0,2,1:T(8,128)(2,1)} %bitcast.194) | data formatting | bytes 8388608 | tf_op jit(solution)/shard_map/reshape | solution.py:187
  551.3 4.9 reduce_sum.62
  556.1 3.2 fusion.35
  563.8 5.4 fusion.24
  570.2 6.8 %all-to-all-start.3 = ((bf16[8,128,768]{1,2,0:T(8,128)(2,1)}), bf16[8,128,768]{1,2,0:T(8,128)(2,1)S(1)}, u32[]{:S(2)}, u32[]{:S(2)}) async-start(bf16[8,128,768]{1,2,0:T(8,128)(2,1)} %bitcast.198), calls=%async_computation.3 | async-start | bytes 3145728 | tf_op jit(solution)/shard_map/all_to_all | solution.py:19
  579.1 6.1 %fusion.28 = bf16[256,2,128]{2,0,1:T(8,128)(2,1)} fusion(bf16[128,6144]{1,0:T(8,128)(2,1)S(1)} %copy-done, bf16[256,2,1024]{2,0,1:T(8,128)(2,1)} %copy.78, bf16[256,2,1024]{2,0,1:T(8,128)(2,1)} %copy.77, bf16[256,2,4096]{2,0,1:T(8,128)(2,1)} %copy.60), kind=kOutput, calls=%fused_computation.52 | convolution fusion | flops 824246272 | bytes 7995392 | tf_op jit(solution)/shard_map/irc,nc->rin/dot_general | solution.py:201
  585.2 12.4 %all-to-all-done.3 = bf16[8,128,768]{1,2,0:T(8,128)(2,1)S(1)} async-done(((bf16[8,128,768]{1,2,0:T(8,128)(2,1)}), bf16[8,128,768]{1,2,0:T(8,128)(2,1)S(1)}, u32[]{:S(2)}, u32[]{:S(2)}) %all-to-all-start.3) | async-done | bytes 1572896 | tf_op jit(solution)/shard_map/all_to_all | solution.py:19
  (263 shorter events, 155.9 us)
Async XLA Ops:
  7.2 572.0 %copy-start = (bf16[128,6144]{1,0:T(8,128)(2,1)S(1)}, bf16[128,6144]{1,0:T(8,128)(2,1)}, u32[]{:S(2)}) copy-start(bf16[128,6144]{1,0:T(8,128)(2,1)} %param.27) | copy-start | bytes 4718596
  7.2 78.9 %all-gather.4.cloned.1.call-start = ((), (), s32[]{:S(2)}) async-start(), calls=%async_computation.4 | async-start | bytes 4325376 | tf_op jit(solution)/shard_map/all_gather | solution.py:58
  7.9 163.8 %all-gather.6.cloned.1.call-start = ((), (), s32[]{:S(2)}) async-start(), calls=%async_computation.5 | async-start | bytes 8912896 | tf_op jit(solution)/shard_map/all_gather | solution.py:25
  397.0 31.6 %all-to-all-start = ((bf16[16,256,256]{1,2,0:T(8,128)(2,1)}), bf16[16,256,256]{1,2,0:T(8,128)(2,1)}, u32[]{:S(2)}, u32[]{:S(2)}) async-start(bf16[16,256,256]{1,2,0:T(8,128)(2,1)} %convert_element_type.58), calls=%async_computation | async-start | bytes 4194304 | tf_op jit(solution)/shard_map/all_to_all | solution.py:180
  405.1 59.6 %copy-start.2 = (bf16[512,256]{1,0:T(8,128)(2,1)S(1)}, bf16[512,256]{1,0:T(8,128)(2,1)}, u32[]{:S(2)}) copy-start(bf16[512,256]{1,0:T(8,128)(2,1)} %param.23) | copy-start | bytes 786436
  428.6 33.5 %all-to-all-start.1 = ((bf16[16,256,256]{1,2,0:T(8,128)(2,1)}), bf16[16,256,256]{1,2,0:T(8,128)(2,1)}, u32[]{:S(2)}, u32[]{:S(2)}) async-start(bf16[16,256,256]{1,2,0:T(8,128)(2,1)} %convert_element_type.59), calls=%async_computation.1 | async-start | bytes 4194304 | tf_op jit(solution)/shard_map/all_to_all | solution.py:19
  433.1 106.0 %all-gather.8.cloned.1.call-start = ((), (), s32[]{:S(2)}) async-start(), calls=%async_computation.6 | async-start | bytes 8650752 | tf_op jit(solution)/shard_map/all_gather | solution.py:25
  468.1 101.1 %all-to-all-start.2 = ((bf16[8,256,256]{1,2,0:T(8,128)(2,1)}), bf16[8,256,256]{1,2,0:T(8,128)(2,1)S(1)}, u32[]{:S(2)}, u32[]{:S(2)}) async-start(bf16[8,256,256]{1,2,0:T(8,128)(2,1)} %bitcast.199), calls=%async_computation.2 | async-start | bytes 2097152 | tf_op jit(solution)/shard_map/all_to_all | solution.py:19
  556.1 7.7 %copy-start.3 = (bf16[512,128]{1,0:T(8,128)(2,1)S(1)}, bf16[512,128]{1,0:T(8,128)(2,1)}, u32[]{:S(2)}) copy-start(bf16[512,128]{1,0:T(8,128)(2,1)} %param.19) | copy-start | bytes 393220
  569.2 1.0 copy-start.1
  570.2 27.3 %all-to-all-start.3 = ((bf16[8,128,768]{1,2,0:T(8,128)(2,1)}), bf16[8,128,768]{1,2,0:T(8,128)(2,1)S(1)}, u32[]{:S(2)}, u32[]{:S(2)}) async-start(bf16[8,128,768]{1,2,0:T(8,128)(2,1)} %bitcast.198), calls=%async_computation.3 | async-start | bytes 3145728 | tf_op jit(solution)/shard_map/all_to_all | solution.py:19
Sparse Core Ops, SparseCore 0:
  9.8 76.3 all-gather.3
  88.7 83.0 all-gather.5
  464.9 74.2 all-gather.7
where the time goes:
time: 611 us; the launch traced here: 605 us
  waiting for transfers between devices  290 us (47%)
  local copies, waits for them, and re-layouts  145 us (24%)
  other arithmetic  61.1 us (10%)
  matrix products  42.8 us (7%)
  loops' own time  32.5 us (5%)
  starting transfers between devices  19.6 us (3%)
  between operations  13.9 us (2%)
    all_gather x2, waiting for transfers between devices, in_one_piece(): out, at, done = (lax.all_gather(both, axis, axis=dim, tiled=True), 0, [])  151 us
    all_gather x1, waiting for transfers between devices, local(): full_grad = lax.all_gather(out_grad, ('role', 'tp'), axis=1, tiled=True)  75.8 us
    all_to_all x3, waiting for transfers between devices, sum_at_owner(): lax.all_to_all(tiles, axis, split_axis=0, concat_axis=0, tiled=True)  39.3 us
    another operation x21, local copies, waits for them, and re-layouts  32.8 us
    another operation x1, loops' own time, attend_side(): return lax.fori_loop(0, block_count, slot_turn, empty_side())  31.7 us
    all_to_all x1, waiting for transfers between devices, local(): lax.all_to_all(query_acc.astype(jnp.bfloat16), ('role', 'wide'), split_ax...  23.5 us
    dynamic_update_slice x10, other arithmetic, tile(): lax.dynamic_update_index_in_dim(kv_acc, current + tile_kv, target, 0)  17 us
    dynamic_slice x16, local copies, waits for them, and re-layouts, tile(): lax.dynamic_slice_in_dim(grad_all, block_q * row_halves, row_halves, 0)  15.8 us
  transfers between devices with their start and end apart: 7, of which 6 were waited for; matrix products, arithmetic and copies ran while one was open for 8% of the time, Pallas kernels for 0%

commit v1 on v0

--- a/solution.py
+++ b/solution.py
@@ -55,7 +55,12 @@
     score_scale = HEAD_SIZE ** (-0.5)
     total_rows = wide_count * local_rows
     block_count = tasks.shape[1]
-    full_grad = lax.all_gather(out_grad, ("role", "tp"), axis=1, tiled=True)
+    kept_rows = []
+    for _ in range(jax.lax.psum(1, ("role", "tp"))):
+        kept_rows.append(out_grad)
+    full_grad = jnp.concatenate(
+        jax.lax.all_to_all(jnp.stack(kept_rows, axis=0), ("role", "tp"), 0, 0), 1
+    )
     grad_half = lax.dynamic_slice_in_dim(full_grad, role_pos * (D // 2), D // 2, 1)
     out_part = lax.dot_general(
         attn_out, grad_half, (((0,), (0,)), ((), ())), preferred_element_type=jnp.float32

time: 611 us -> 650 us (1.064)
  waiting for transfers between devices: 290 us -> 310 us
  starting transfers between devices: 19.6 us -> 30.8 us
  local copies, waits for them, and re-layouts: 145 us -> 153 us
    all_to_all x0 -> x1, waiting for transfers between devices: none -> 95.8 us  [local(): jax.lax.all_to_all(jnp.stack(kept_rows, axis=0), ('role', 'tp'), 0, 0)]
    all_gather x1 -> x0, waiting for transfers between devices: 75.8 us -> none  [local(): full_grad = lax.all_gather(out_grad, ('role', 'tp'), axis=1, tiled=True)]
    all_to_all x0 -> x1, starting transfers between devices: none -> 11.2 us  [local(): jax.lax.all_to_all(jnp.stack(kept_rows, axis=0), ('role', 'tp'), 0, 0)]
    another operation x21 -> x22, local copies, waits for them, and re-layouts: 32.8 us -> 36.6 us
where the time goes in v1:
time: 650 us; the launch traced here: 644 us
  waiting for transfers between devices  310 us (48%)
  local copies, waits for them, and re-layouts  153 us (24%)
  other arithmetic  61.4 us (9%)
  matrix products  42.7 us (7%)
  loops' own time  31.4 us (5%)
  starting transfers between devices  30.8 us (5%)
  between operations  14.2 us (2%)
    all_gather x2, waiting for transfers between devices, in_one_piece(): out, at, done = (lax.all_gather(both, axis, axis=dim, tiled=True), 0, [])  152 us
    all_to_all x1, waiting for transfers between devices, local(): jax.lax.all_to_all(jnp.stack(kept_rows, axis=0), ('role', 'tp'), 0, 0)  95.8 us
    all_to_all x3, waiting for transfers between devices, sum_at_owner(): lax.all_to_all(tiles, axis, split_axis=0, concat_axis=0, tiled=True)  39.4 us
    another operation x21, local copies, waits for them, and re-layouts  32.7 us
    another operation x1, loops' own time, attend_side(): return lax.fori_loop(0, block_count, slot_turn, empty_side())  30.6 us
    all_to_all x1, waiting for transfers between devices, local(): lax.all_to_all(query_acc.astype(jnp.bfloat16), ('role', 'wide'), split_ax...  23.4 us
    dynamic_update_slice x10, other arithmetic, tile(): lax.dynamic_update_index_in_dim(kv_acc, current + tile_kv, target, 0)  17 us
    dynamic_slice x16, local copies, waits for them, and re-layouts, tile(): lax.dynamic_slice_in_dim(grad_all, block_q * row_halves, row_halves, 0)  15.8 us
  transfers between devices with their start and end apart: 7, of which 6 were waited for; matrix products, arithmetic and copies ran while one was open for 8% of the time, Pallas kernels for 0%

profile of v1, /device:TPU:1, one launch (start us, length us, event | category | flops | bytes accessed | tf_op | source)
XLA Modules:
  0.0 644.3 jit_solution(11085544233110148538)
XLA Ops:
  7.2 4.0 stack.2
  11.1 11.2 %all-to-all-start = ((bf16[32,512,128]{2,1,0:T(8,128)(2,1)}), bf16[32,512,128]{2,1,0:T(8,128)(2,1)}, u32[]{:S(2)}, u32[]{:S(2)}) async-start(bf16[32,512,128]{2,1,0:T(8,128)(2,1)} %stack.2), calls=%async_computation | async-start | bytes 8388608 | tf_op jit(solution)/shard_map/all_to_all | solution.py:62
  23.9 95.8 %all-to-all-done = bf16[32,512,128]{2,1,0:T(8,128)(2,1)} async-done(((bf16[32,512,128]{2,1,0:T(8,128)(2,1)}), bf16[32,512,128]{2,1,0:T(8,128)(2,1)}, u32[]{:S(2)}, u32[]{:S(2)}) %all-to-all-start) | async-done | bytes 4194336 | tf_op jit(solution)/shard_map/all_to_all | solution.py:62
  119.7 6.5 %copy.70 = bf16[32,512,128]{1,2,0:T(8,128)(2,1)} copy(bf16[32,512,128]{2,1,0:T(8,128)(2,1)} %all-to-all-done) | data formatting | bytes 8388608 | tf_op jit(solution)/shard_map/all_to_all | solution.py:62
  127.2 84.4 %all-gather.3.cloned.1.call-done = bf16[8192,512]{0,1:T(8,128)(2,1)} async-done(((bf16[512,512]{0,1:T(8,128)(2,1)}), bf16[8192,512]{0,1:T(8,128)(2,1)}) %all-gather.3.cloned.1.call-update) | async-done | bytes 8388624 | tf_op jit(solution)/shard_map/all_gather | solution.py:25
  211.6 3.2 slice.52
  214.8 4.1 convert.5
  218.9 213.0 %conditional.3 = (f32[16,256,256]{1,2,0:T(8,128)}, f32[16,256,256]{1,2,0:T(8,128)}) conditional(s32[]{:T(128)} %convert_element_type.57, (s32[]{:T(128)}, s32[8,16,2]{1,2,0:T(2,128)}, s32[4096]{0:T(1024)}, bf16[8192,512]{0,1:T(8,128)(2,1)}, f32[2,4096]{1,0:T(2,128)}, /*index=5*/bf16[4096,256]{0,1:T(8,128)(2,1)}, f32[2,4096,128]{1,2,0:T(8,128)}, ...), branch_computations={%region_2.7_spmd.clone, %region_7.8_spmd} | conditional | flops 172417568 | bytes 72474416 | solution.py:182
  219.6 3.2 slice.49
  222.7 4.5 reshape.203
  227.2 6.8 %fusion.23 = f32[2,4096]{1,0:T(2,128)S(1)} fusion(bf16[2,4096,128]{1,0,2:T(2,128)(2,1)} %reshape.203, f32[2,4096,128]{1,2,0:T(8,128)} %get-tuple-element.645), kind=kLoop, calls=%fused_computation.43 | loop fusion | flops 3137536 | bytes 6324224 | tf_op jit(solution)/shard_map/irpd,ripd->rpi/dot_general | solution.py:92
  237.2 11.5 %copy.104 = bf16[8192,512]{1,0:T(8,128)(2,1)} copy(bf16[8192,512]{0,1:T(8,128)(2,1)} %get-tuple-element.646) | data formatting | bytes 16777216 | tf_op jit(solution)/shard_map
  250.0 11.6 %copy.103 = bf16[8192,512]{1,0:T(8,128)(2,1)} copy(bf16[8192,512]{0,1:T(8,128)(2,1)} %get-tuple-element.646) | data formatting | bytes 16777216 | tf_op jit(solution)/shard_map
  268.7 163.2 %while.56 = (s32[]{:T(128)}, f32[16,256,256]{1,2,0:T(8,128)}, f32[16,256,256]{1,2,0:T(8,128)}, s32[16,2]{0,1:T(2,128)S(1)}, s32[4096]{0:T(1024)}, /*index=5*/bf1...) while((s32[]{:T(128)}, f32[16,256,256]{1,2,0:T(8,128)}, ...), condition=%wide.region_6.6_spmd, body=%wide.region_3.5_spmd.sunk | while | flops 169280032 | bytes 7429371 | solution.py:180
  274.6 55.2 %while.57 = (s32[]{:T(128)}, f32[256,256]{0,1:T(8,128)S(1)}, f32[16,256,256]{1,2,0:T(8,128)}, s32[]{:T(128)}, bf16[4096,128]{1,0:T(8,128)(2,1)}, /*index=5*/s32[...) while((s32[]{:T(128)}, f32[256,256]{0,1:T(8,128)S(1)}, ...), condition=%wide.region_5.4_spmd, body=%wide.region_4.3_spmd.sunk | while | flops 169214464 | bytes 5321220 | solution.py:174
  431.8 3.8 convert_element_type.58
  435.6 4.3 all-to-all-start.1
  440.0 3.8 convert_element_type.59
  443.8 23.4 %all-to-all-done.1 = bf16[16,256,256]{1,2,0:T(8,128)(2,1)} async-done(((bf16[16,256,256]{1,2,0:T(8,128)(2,1)}), bf16[16,256,256]{1,2,0:T(8,128)(2,1)}, u32[]{:S(2)}, u32[]{:S(2)}) %all-to-all-start.1) | async-done | bytes 2097184 | tf_op jit(solution)/shard_map/all_to_all | solution.py:185
  467.2 4.5 all-to-all-start.2
  473.6 27.1 %all-to-all-done.2 = bf16[16,256,256]{1,2,0:T(8,128)(2,1)} async-done(((bf16[16,256,256]{1,2,0:T(8,128)(2,1)}), bf16[16,256,256]{1,2,0:T(8,128)(2,1)}, u32[]{:S(2)}, u32[]{:S(2)}) %all-to-all-start.2) | async-done | bytes 2097184 | tf_op jit(solution)/shard_map/all_to_all | solution.py:19
  503.3 3.3 convolution_convert_fusion.1
  506.6 3.7 all-to-all-start.3
  510.3 67.4 %all-gather.5.cloned.1.call-done = bf16[512,8192]{0,1:T(8,128)(2,1)} async-done(((bf16[512,256]{0,1:T(8,128)(2,1)}), bf16[512,8192]{0,1:T(8,128)(2,1)}) %all-gather.5.cloned.1.call-update) | async-done | bytes 8388624 | tf_op jit(solution)/shard_map/all_gather | solution.py:25
  577.7 5.7 fusion.34
  583.4 6.4 copy.80
  589.8 4.9 reduce_sum.62
  594.7 3.2 fusion.35
  602.4 5.4 fusion.24
  608.8 6.9 %all-to-all-start.4 = ((bf16[8,128,768]{1,2,0:T(8,128)(2,1)}), bf16[8,128,768]{1,2,0:T(8,128)(2,1)S(1)}, u32[]{:S(2)}, u32[]{:S(2)}) async-start(bf16[8,128,768]{1,2,0:T(8,128)(2,1)} %bitcast.204), calls=%async_computation.4 | async-start | bytes 3145728 | tf_op jit(solution)/shard_map/all_to_all | solution.py:19
  617.9 6.1 fusion.28
  624.0 12.4 %all-to-all-done.4 = bf16[8,128,768]{1,2,0:T(8,128)(2,1)S(1)} async-done(((bf16[8,128,768]{1,2,0:T(8,128)(2,1)}), bf16[8,128,768]{1,2,0:T(8,128)(2,1)S(1)}, u32[]{:S(2)}, u32[]{:S(2)}) %all-to-all-start.4) | async-done | bytes 1572896 | tf_op jit(solution)/shard_map/all_to_all | solution.py:19
  (268 shorter events, 160.2 us)
Async XLA Ops:
  7.2 610.8 %copy-start = (bf16[128,6144]{1,0:T(8,128)(2,1)S(1)}, bf16[128,6144]{1,0:T(8,128)(2,1)}, u32[]{:S(2)}) copy-start(bf16[128,6144]{1,0:T(8,128)(2,1)} %param.27) | copy-start | bytes 4718596
  11.1 11.3 %copy-start.2 = (bf16[512,256]{1,0:T(8,128)(2,1)S(1)}, bf16[512,256]{1,0:T(8,128)(2,1)}, u32[]{:S(2)}) copy-start(bf16[512,256]{1,0:T(8,128)(2,1)} %param.23) | copy-start | bytes 786436
  11.1 108.6 %all-to-all-start = ((bf16[32,512,128]{2,1,0:T(8,128)(2,1)}), bf16[32,512,128]{2,1,0:T(8,128)(2,1)}, u32[]{:S(2)}, u32[]{:S(2)}) async-start(bf16[32,512,128]{2,1,0:T(8,128)(2,1)} %stack.2), calls=%async_computation | async-start | bytes 8388608 | tf_op jit(solution)/shard_map/all_to_all | solution.py:62
  22.4 189.2 %all-gather.3.cloned.1.call-start = ((), (), s32[]{:S(2)}) async-start(), calls=%async_computation.5 | async-start | bytes 8912896 | tf_op jit(solution)/shard_map/all_gather | solution.py:25
  23.9 102.3 %copy-start.4 = (bf16[512,256]{1,0:T(8,128)(2,1)S(1)}, bf16[512,256]{1,0:T(8,128)(2,1)}, u32[]{:S(2)}) copy-start(bf16[512,256]{1,0:T(8,128)(2,1)} %param.20) | copy-start | bytes 786436
  435.6 31.5 %all-to-all-start.1 = ((bf16[16,256,256]{1,2,0:T(8,128)(2,1)}), bf16[16,256,256]{1,2,0:T(8,128)(2,1)}, u32[]{:S(2)}, u32[]{:S(2)}) async-start(bf16[16,256,256]{1,2,0:T(8,128)(2,1)} %convert_element_type.58), calls=%async_computation.1 | async-start | bytes 4194304 | tf_op jit(solution)/shard_map/all_to_all | solution.py:185
  443.8 59.6 %copy-start.3 = (bf16[512,256]{1,0:T(8,128)(2,1)S(1)}, bf16[512,256]{1,0:T(8,128)(2,1)}, u32[]{:S(2)}) copy-start(bf16[512,256]{1,0:T(8,128)(2,1)} %param.23) | copy-start | bytes 786436
  467.2 33.5 %all-to-all-start.2 = ((bf16[16,256,256]{1,2,0:T(8,128)(2,1)}), bf16[16,256,256]{1,2,0:T(8,128)(2,1)}, u32[]{:S(2)}, u32[]{:S(2)}) async-start(bf16[16,256,256]{1,2,0:T(8,128)(2,1)} %convert_element_type.59), calls=%async_computation.2 | async-start | bytes 4194304 | tf_op jit(solution)/shard_map/all_to_all | solution.py:19
  471.7 106.0 %all-gather.5.cloned.1.call-start = ((), (), s32[]{:S(2)}) async-start(), calls=%async_computation.6 | async-start | bytes 8650752 | tf_op jit(solution)/shard_map/all_gather | solution.py:25
  506.6 101.2 %all-to-all-start.3 = ((bf16[8,256,256]{1,2,0:T(8,128)(2,1)}), bf16[8,256,256]{1,2,0:T(8,128)(2,1)S(1)}, u32[]{:S(2)}, u32[]{:S(2)}) async-start(bf16[8,256,256]{1,2,0:T(8,128)(2,1)} %bitcast.200), calls=%async_computation.3 | async-start | bytes 2097152 | tf_op jit(solution)/shard_map/all_to_all | solution.py:19
  594.7 7.7 %copy-start.5 = (bf16[512,128]{1,0:T(8,128)(2,1)S(1)}, bf16[512,128]{1,0:T(8,128)(2,1)}, u32[]{:S(2)}) copy-start(bf16[512,128]{1,0:T(8,128)(2,1)} %param.19) | copy-start | bytes 393220
  607.8 1.0 copy-start.1
  608.8 27.5 %all-to-all-start.4 = ((bf16[8,128,768]{1,2,0:T(8,128)(2,1)}), bf16[8,128,768]{1,2,0:T(8,128)(2,1)S(1)}, u32[]{:S(2)}, u32[]{:S(2)}) async-start(bf16[8,128,768]{1,2,0:T(8,128)(2,1)} %bitcast.204), calls=%async_computation.4 | async-start | bytes 3145728 | tf_op jit(solution)/shard_map/all_to_all | solution.py:19
Sparse Core Ops, SparseCore 0:
  127.4 84.1 all-gather.2
  503.4 74.2 all-gather.4
